TPU v7x, 32 devices: a whole 2x2x4 slice. The times are simulated.
32 devices in a mesh: leaf: 32 (over z, y, x, core).
Axes of the slice: x: 2, y: 2, z: 4, core: 2. Of those that a mesh axis runs over, the one named last changes fastest.
Arguments:
- coords: float32 [3, 262144], P(None, 'leaf'), may hold values from 0 to 1
- charges: bfloat16 [262144, 128], P('leaf'), may hold values from -6 to 6
- near_leaves: int32 [2048, 27], P('leaf'), may hold values from 0 to 191
- leaf_basis: bfloat16 [2048, 4096], P('leaf'), may hold values from -1 to 1
- leaf_transfer: bfloat16 [2048, 1024], P('leaf'), may hold values from -0.75 to 0.75
- mid_transfer: bfloat16 [256, 1024], P('leaf'), may hold values from -0.75 to 0.75
- base_transfer: bfloat16 [32, 1024], P('leaf'), may hold values from -0.75 to 0.75
- base_coupling: bfloat16 [6048, 1024], P('leaf'), may hold values from -0.01953125 to 0.01953125
- base_target: int32 [6048, 1], P('leaf'), may hold values from 0 to 31; in each aligned block of 189 rows (0 to 188, 189 to 377, ...) at most 11 rows name the same one
- base_source: int32 [6048], P('leaf'), may hold values from 0 to 31
- top_coupling: bfloat16 [256, 1024], P('leaf'), may hold values from -0.015625 to 0.015625
- top_target: int32 [256], P('leaf'), may hold values from 0 to 3
- top_source: int32 [256], P('leaf'), may hold values from 0 to 3
Outputs:
- potential: bfloat16 [262144, 128], P('leaf')
Inputs may be any that keep to these rules, and one draw needn't show every extreme that they name: `near_leaves`: entry j of leaf l names leaf 64 * (l // 64 - 1) + j: a leaf of the device before in Morton order, of the row's own device, or of the device after; repeats may occur. `base_target`: among the 189 blocks of one device no base cluster is the target more than 11 times; that count is reached.
All inputs are finite; a program needn't handle non-finite values.
Results may differ from a plain program's by a relative error of at most 0.01.
Values may be sent and summed in bfloat16 or wider, within the bound.
A program may use at most 128 MiB of HBM per device.

v0:
```python
import math
import jax
import jax.numpy as jnp
from jax import lax
from jax.sharding import PartitionSpec as P

K = 32
RHS = 128
M = 128
NB = 189
delta_sq = 0.0025


def extended(array, sides, width):
    for axis, dim in sides:
        size, length = (lax.axis_size(axis), array.shape[dim])
        up = [(i, (i + 1) % size) for i in range(size - 1)]
        down = [(j, i) for i, j in up]
        last = lax.slice_in_dim(array, length - width, length, axis=dim)
        first = lax.slice_in_dim(array, 0, width, axis=dim)
        before = lax.ppermute(last, axis, up)
        after = lax.ppermute(first, axis, down)
        array = jnp.concatenate([before, array, after], axis=dim)
    return array


def near_block(points, pool_points, pool_charges, columns):
    near_scale = 1.0 / math.sqrt(columns.shape[1] * points.shape[2])

    def near_step(running, column):
        other_points = jnp.take(pool_points, column, axis=1)
        other_charges = jnp.take(pool_charges, column, axis=0)
        squares = jnp.sum((points[:, :, :, None] - other_points[:, :, None, :]) ** 2, axis=0)
        kernel = (near_scale / jnp.sqrt(squares + delta_sq)).astype(jnp.bfloat16)
        update = jnp.einsum(
            "lab,lbr->lar", kernel, other_charges, preferred_element_type=jnp.float32
        )
        return (running + update, None)

    initial = jnp.zeros((points.shape[1], points.shape[2], pool_charges.shape[2]), jnp.float32)
    running, unused = lax.scan(near_step, initial, columns.T)
    return running


def per_device(
    coords,
    charges,
    near_leaves,
    leaf_basis,
    leaf_transfer,
    mid_transfer,
    base_transfer,
    base_coupling,
    base_target,
    base_source,
    top_coupling,
    top_target,
    top_source,
):
    single_precision = jnp.float32
    bf16 = jnp.bfloat16
    leaves = leaf_basis.shape[0]
    mid_count = leaves // 8
    base_count = leaves // 64
    devices = lax.axis_size("leaf")
    position = lax.axis_index("leaf")
    charge_row_block = charges.reshape(leaves, M, RHS)
    own_points = coords.reshape(3, leaves, M)
    point_rows = own_points.transpose(1, 0, 2).reshape(leaves, 3 * M)
    pool_points = (
        extended(point_rows, (("leaf", 0),), leaves).reshape(3 * leaves, 3, M).transpose(1, 0, 2)
    )
    pool_charges = extended(
        charge_row_block.reshape(leaves, M * RHS), (("leaf", 0),), leaves
    ).reshape(3 * leaves, M, RHS)
    basis_matrix = leaf_basis.reshape(leaves, K, M)
    leaf_coefficients = jnp.einsum(
        "xpt,xtu->xpu", basis_matrix, charge_row_block, preferred_element_type=single_precision
    ).astype(bf16)
    mid_coeffs = jnp.einsum(
        "mckp,mckr->mpr",
        leaf_transfer.reshape(mid_count, 8, K, K),
        leaf_coefficients.reshape(mid_count, 8, K, RHS),
        preferred_element_type=single_precision,
    ).astype(bf16)
    base_coeffs = jnp.einsum(
        "mckp,mckr->mpr",
        mid_transfer.reshape(base_count, 8, K, K),
        mid_coeffs.reshape(base_count, 8, K, RHS),
        preferred_element_type=single_precision,
    ).astype(bf16)
    base_lift = base_transfer.reshape(base_count, K, K)
    lifted = jnp.einsum(
        "bkp,bkr->bpr", base_lift, base_coeffs, preferred_element_type=single_precision
    ).astype(bf16)
    all_coeffs, all_lifted = (
        lax.all_gather(base_coeffs.reshape(base_count, K * RHS), "leaf", axis=0, tiled=True),
        lax.all_gather(lifted.reshape(base_count, K * RHS), "leaf", axis=0, tiled=True),
    )
    total_bases = base_count * devices
    total_tops = total_bases // 8
    every_base = all_coeffs.reshape(total_bases, K, RHS)
    top_coeffs = jnp.sum(
        all_lifted.reshape(total_tops, 8, K, RHS).astype(single_precision), axis=1
    ).astype(bf16)
    top_products = jnp.einsum(
        "bts,bsr->btr",
        top_coupling.reshape(-1, K, K),
        jnp.take(top_coeffs, top_source, axis=0),
        preferred_element_type=single_precision,
    )
    top_partial = jax.ops.segment_sum(top_products, top_target, num_segments=total_tops)
    top_sum = lax.psum(top_partial, "leaf")
    top_field = top_sum.astype(bf16)
    targets = base_target[:, 0]
    per_cluster = max(2, 2 * NB // devices)
    per_owner = per_cluster * base_count
    owners = targets // base_count
    onehot = (owners[:, None] == jnp.arange(devices, dtype=jnp.int32)[None, :]).astype(jnp.int32)
    earlier = jnp.cumsum(onehot, axis=0) - onehot
    slot_index = jnp.sum(earlier * onehot, axis=1)
    placed = owners * per_owner + slot_index
    send_blocks = jnp.zeros((devices * per_owner, K * K), bf16).at[placed].set(base_coupling)
    labels = base_source * base_count + (targets - owners * base_count)
    send_labels = jnp.full((devices * per_owner,), -1, jnp.int32).at[placed].set(labels)
    sent = (send_blocks.reshape(devices, per_owner, K * K), send_labels.reshape(devices, per_owner))
    blocks = lax.all_to_all(sent[0], "leaf", split_axis=0, concat_axis=0, tiled=True)
    got_labels = lax.all_to_all(sent[1], "leaf", split_axis=0, concat_axis=0, tiled=True)
    present = got_labels >= 0
    source_ids = jnp.where(present, got_labels // base_count, 0)
    gathered = jnp.take(every_base, source_ids, axis=0)
    shaped = blocks.reshape(blocks.shape[0], blocks.shape[1], K, K)
    result = jnp.einsum(
        "dnts,dnsr->dntr", shaped, gathered, preferred_element_type=single_precision
    )
    results, got_labels = (result, got_labels)
    local_ids = jnp.where(got_labels >= 0, got_labels % base_count, base_count).reshape(-1)
    coupled = jax.ops.segment_sum(results.reshape(-1, K, RHS), local_ids, num_segments=base_count)
    my_bases = position * base_count + jnp.arange(base_count, dtype=jnp.int32)
    top_mine = jnp.take(top_field, my_bases // 8, axis=0)
    base_field = (
        coupled
        + jnp.einsum("bkp,bpr->bkr", base_lift, top_mine, preferred_element_type=single_precision)
    ).astype(bf16)
    mid_field = jnp.einsum(
        "mkp,mpr->mkr",
        mid_transfer.reshape(mid_count, K, K),
        jnp.repeat(base_field, 8, axis=0),
        preferred_element_type=single_precision,
    ).astype(bf16)
    leaf_potential = jnp.einsum(
        "lkp,lpr->lkr",
        leaf_transfer.reshape(leaves, K, K),
        jnp.repeat(mid_field, 8, axis=0),
        preferred_element_type=single_precision,
    ).astype(bf16)
    near_field = near_block(own_points, pool_points, pool_charges, near_leaves)
    distant_field = jnp.einsum(
        "cbz,cbw->czw", basis_matrix, leaf_potential, preferred_element_type=single_precision
    )
    return (near_field + distant_field).astype(bf16).reshape(leaves * M, RHS)


def solution(mesh):
    in_specs = (
        P(None, "leaf"),
        P("leaf", None),
        P("leaf", None),
        P("leaf", None),
        P("leaf", None),
        P("leaf", None),
        P("leaf", None),
        P("leaf", None),
        P("leaf", None),
        P("leaf"),
        P("leaf", None),
        P("leaf"),
        P("leaf"),
    )
    out_specs = P("leaf", None)
    return jax.shard_map(
        per_device, mesh=mesh, in_specs=in_specs, out_specs=out_specs, check_vma=False
    )
```

profile of v0, /device:TPU:0, one launch (start us, length us, event | category | flops | bytes accessed | tf_op | source)
XLA Modules:
  0.0 797.9 jit_solution(6871703731802868991)
XLA Ops:
  21.0 8.4 %all-to-all-start = ((s32[32,1,11]{2,1,0:T(1,128)}), s32[32,1,11]{2,1,0:T(1,128)S(1)}, u32[]{:S(2)}, u32[]{:S(2)}) async-start(s32[32,1,11]{2,1,0:T(1,128)} %bitcast.22), calls=%async_computation | async-start | bytes 32768 | tf_op jit(solution)/shard_map/all_to_all | solution.py:128
  33.9 64.6 %all-gather = bf16[32,1,4096]{2,1,0:T(2,128)(2,1)S(1)} all-gather(bf16[1,1,4096]{2,1,0:T(2,128)(2,1)S(1)} %reshape.358), channel_id=1, replica_groups=mesh['leaf'=32] {'leaf'}, dimensions={0}, use_global_device_ids=true | all-gather | bytes 270336 | tf_op jit(solution)/shard_map/all_gather | solution.py:98
  102.0 38.0 %all-gather.1 = bf16[32,1,4096]{2,1,0:T(2,128)(2,1)S(1)} all-gather(bf16[1,1,4096]{2,1,0:T(2,128)(2,1)S(1)} %reshape.360), channel_id=1, replica_groups=mesh['leaf'=32] {'leaf'}, dimensions={0}, use_global_device_ids=true | all-gather | bytes 270336 | tf_op jit(solution)/shard_map/all_gather | solution.py:97
  158.2 40.9 %psum.7 = bf16[4,32,128]{2,1,0:T(8,128)(2,1)S(1)} all-reduce(f32[4,32,128]{2,1,0:T(8,128)S(1)} %scatter_fusion), channel_id=1, replica_groups=mesh['leaf'=32] {'leaf'}, use_global_device_ids=true, to_apply=%region_5.6 | all-reduce | flops 16384 | bytes 98304 | tf_op jit(solution)/shard_map/psum | solution.py:113
  219.1 31.1 %scatter_fusion.1 = f32[32,128,1]{1,0,2:T(8,128)S(1)} fusion(f32[32,128,1]{1,0,2:T(8,128)S(1)} %convolution_bitcast_fusion.2, s32[352]{0:T(512)S(1)} %reshape.354, f32[352,32,128]{2,1,0:T(8,128)} %bitcast.136), kind=kCustom, calls=%fused_computation.7 | custom fusion | flops 1441792 | bytes 17302912 | tf_op jit(solution)/shard_map/scatter-add | solution.py:138
  260.5 532.9 %while.12 = (s32[]{:T(128)}, f32[64,128,128]{2,1,0:T(8,128)}, f32[3,8192]{1,0:T(4,128)S(1)}, s32[27,64]{1,0:T(8,128)}, f32[3,192,128]{2,0,1:T(4,128)}, /*index=5*/bf16[192,128,128]{2,1,0:T(8,128)(2,1)}, s32[]{:T(128)}, s32[]{:T(128)}) while((s32[]{:T(128)}, f32[64,128,128]{2,1,0:T(8,128)}, f32[3,8192]{1,0:T(4,128)S(1)}, ...), condition=%wide.region_2.3_spmd.clone, body=%wide.region_0.2_spmd.clone.sunk | while | flops 283141696 | bytes 24057648 | solution.py:41
  263.8 6.2 multiply_reduce_fusion.2
  282.3 6.2 multiply_reduce_fusion.2
  292.2 6.6 select_add_fusion.2
  302.1 6.2 multiply_reduce_fusion.2
  312.0 6.6 select_add_fusion.2
  321.8 6.2 multiply_reduce_fusion.2
  331.8 6.6 select_add_fusion.2
  341.6 6.2 multiply_reduce_fusion.2
  351.6 6.6 select_add_fusion.2
  361.4 6.2 multiply_reduce_fusion.2
  371.4 6.6 select_add_fusion.2
  381.2 6.2 multiply_reduce_fusion.2
  391.2 6.6 select_add_fusion.2
  401.0 6.2 multiply_reduce_fusion.2
  410.9 6.6 select_add_fusion.2
  420.8 6.2 multiply_reduce_fusion.2
  430.7 6.6 select_add_fusion.2
  440.5 6.2 multiply_reduce_fusion.2
  450.5 6.6 select_add_fusion.2
  460.3 6.2 multiply_reduce_fusion.2
  470.3 6.6 select_add_fusion.2
  480.1 6.2 multiply_reduce_fusion.2
  490.1 6.6 select_add_fusion.2
  499.9 6.2 multiply_reduce_fusion.2
  509.8 6.6 select_add_fusion.2
  519.7 6.2 multiply_reduce_fusion.2
  529.6 6.6 select_add_fusion.2
  539.5 6.2 multiply_reduce_fusion.2
  549.4 6.6 select_add_fusion.2
  569.2 6.6 select_add_fusion.2
  589.0 6.6 select_add_fusion.2
  608.8 6.6 select_add_fusion.2
  628.5 6.6 select_add_fusion.2
  648.3 6.6 select_add_fusion.2
  658.1 6.2 multiply_reduce_fusion.2
  668.1 6.6 select_add_fusion.2
  687.9 6.6 select_add_fusion.2
  707.7 6.6 select_add_fusion.2
  727.5 6.6 select_add_fusion.2
  747.2 6.6 select_add_fusion.2
  767.0 6.6 select_add_fusion.2
  786.8 6.6 select_add_fusion.2
  (331 shorter events, 342.6 us)
Async XLA Ops:
  0.0 18.0 %copy-start.13 = (s32[189,1]{0,1:T(1,128)S(1)}, s32[189,1]{0,1:T(1,128)}, u32[]{:S(2)}) copy-start(s32[189,1]{0,1:T(1,128)} %param.23) | copy-start | bytes 2272
  0.0 29.5 %copy-start.7 = (bf16[64,4096]{1,0:T(8,128)(2,1)S(1)}, bf16[64,4096]{1,0:T(8,128)(2,1)}, u32[]{:S(2)}) copy-start(bf16[64,4096]{1,0:T(8,128)(2,1)} %param.18) | copy-start | bytes 1572868
  0.0 29.6 %copy-start.12 = (bf16[8,1024]{1,0:T(8,128)(2,1)S(1)}, bf16[8,1024]{1,0:T(8,128)(2,1)}, u32[]{:S(2)}) copy-start(bf16[8,1024]{1,0:T(8,128)(2,1)} %param.20) | copy-start | bytes 49156
  0.0 29.7 %copy-start.14 = (bf16[1,1024]{1,0:T(2,128)(2,1)S(1)}, bf16[1,1024]{1,0:T(2,128)(2,1)}, u32[]{:S(2)}) copy-start(bf16[1,1024]{1,0:T(2,128)(2,1)} %param.21) | copy-start | bytes 6148
  1.6 28.2 %copy-start.5 = (bf16[64,1024]{1,0:T(8,128)(2,1)S(1)}, bf16[64,1024]{1,0:T(8,128)(2,1)}, u32[]{:S(2)}) copy-start(bf16[64,1024]{1,0:T(8,128)(2,1)} %param.19) | copy-start | bytes 393220
  1.6 28.6 %copy-start = (bf16[8192,128]{1,0:T(8,128)(2,1)S(1)}, bf16[8192,128]{1,0:T(8,128)(2,1)}, u32[]{:S(2)}) copy-start(bf16[8192,128]{1,0:T(8,128)(2,1)} %param.16) | copy-start | bytes 6291460
  1.6 203.9 %collective-permute-start.1 = (f32[64,384]{1,0:T(8,128)}, f32[64,384]{1,0:T(8,128)}, u32[]{:S(2)}, u32[]{:S(2)}) collective-permute-start(f32[64,384]{1,0:T(8,128)} %bitcast.122), channel_id=1, source_target_pairs={{1,0},{2,1},{3,2},{4,3},{5,4},{6,5},{7,6},{8,7},{9,8},{10,9},{11,1... | collective-permute-start | bytes 294920 | tf_op jit(solution)/shard_map/ppermute | solution.py:22
  3.0 203.5 %collective-permute-start = (f32[64,384]{1,0:T(8,128)}, f32[64,384]{1,0:T(8,128)}, u32[]{:S(2)}, u32[]{:S(2)}) collective-permute-start(f32[64,384]{1,0:T(8,128)} %bitcast.122), channel_id=1, source_target_pairs={{0,1},{1,2},{2,3},{3,4},{4,5},{5,6},{6,7},{7,8},{8,9},{9,10},{10,1... | collective-permute-start | bytes 294920 | tf_op jit(solution)/shard_map/ppermute | solution.py:21
  10.9 240.1 %collective-permute-start.3 = (bf16[64,16384]{1,0:T(8,128)(2,1)}, bf16[64,16384]{1,0:T(8,128)(2,1)}, u32[]{:S(2)}, u32[]{:S(2)}) collective-permute-start(bf16[64,16384]{1,0:T(8,128)(2,1)} %reshape_reshape.3), channel_id=1, source_target_pairs={{1,0},{2,1},{3,2},{4,3},{5,4},{6,5},{7,6},{8,7},{9,8},{10,9},{11,1... | collective-permute-start | bytes 6291464 | tf_op jit(solution)/shard_map/ppermute | solution.py:22
  12.2 241.0 %collective-permute-start.2 = (bf16[64,16384]{1,0:T(8,128)(2,1)}, bf16[64,16384]{1,0:T(8,128)(2,1)}, u32[]{:S(2)}, u32[]{:S(2)}) collective-permute-start(bf16[64,16384]{1,0:T(8,128)(2,1)} %reshape_reshape.3), channel_id=1, source_target_pairs={{0,1},{1,2},{2,3},{3,4},{4,5},{5,6},{6,7},{7,8},{8,9},{9,10},{10,1... | collective-permute-start | bytes 6291464 | tf_op jit(solution)/shard_map/ppermute | solution.py:21
  19.0 14.2 %copy-start.15 = (s32[189,1]{0,1:T(1,128)}, s32[189,1]{0,1:T(1,128)S(1)}, u32[]{:S(2)}) copy-start(s32[189,1]{0,1:T(1,128)S(1)} %compare_select_fusion.7) | copy-start | bytes 2272
  21.0 124.0 %all-to-all-start = ((s32[32,1,11]{2,1,0:T(1,128)}), s32[32,1,11]{2,1,0:T(1,128)S(1)}, u32[]{:S(2)}, u32[]{:S(2)}) async-start(s32[32,1,11]{2,1,0:T(1,128)} %bitcast.22), calls=%async_computation | async-start | bytes 32768 | tf_op jit(solution)/shard_map/all_to_all | solution.py:128
  29.7 70.3 %copy-start.3 = (bf16[8,32,32]{2,1,0:T(8,128)(2,1)}, bf16[8,32,32]{2,1,0:T(8,128)(2,1)S(1)}, u32[]{:S(2)}) copy-start(bf16[8,32,32]{2,1,0:T(8,128)(2,1)S(1)} %reshape.231) | copy-start | bytes 49156
  29.8 3.3 copy-start.11
  33.1 0.6 copy-start.10
  100.0 49.0 %copy-start.6 = (bf16[64,1024]{1,0:T(8,128)(2,1)S(1)}, bf16[64,1024]{1,0:T(8,128)(2,1)}, u32[]{:S(2)}) copy-start(bf16[64,1024]{1,0:T(8,128)(2,1)} %param.19) | copy-start | bytes 393220
  145.1 8.8 %copy-start.9 = (s32[32,1,11]{2,1,0:T(1,128)}, s32[32,1,11]{2,1,0:T(1,128)S(1)}, u32[]{:S(2)}) copy-start(s32[32,1,11]{2,1,0:T(1,128)S(1)} %all-to-all-done) | copy-start | bytes 4228
  145.1 63.2 %all-to-all-start.1 = ((bf16[32,11,1024]{2,1,0:T(8,128)(2,1)}), bf16[32,11,1024]{2,1,0:T(8,128)(2,1)}, u32[]{:S(2)}, u32[]{:S(2)}) async-start(bf16[32,11,1024]{2,1,0:T(8,128)(2,1)} %reshape.239), calls=%async_computation.1 | async-start | bytes 2097152 | tf_op jit(solution)/shard_map/all_to_all | solution.py:127
  202.4 5.0 copy-start.1
  219.1 31.1 %copy-start.4 = (bf16[8,32,32]{2,1,0:T(8,128)(2,1)S(1)}, bf16[8,32,32]{2,1,0:T(8,128)(2,1)}, u32[]{:S(2)}) copy-start(bf16[8,32,32]{2,1,0:T(8,128)(2,1)} %copy-done.3) | copy-start | bytes 49156
  260.5 532.9 %copy-start.8 = (bf16[8,32,128]{2,1,0:T(8,128)(2,1)S(1)}, bf16[8,32,128]{2,1,0:T(8,128)(2,1)}, u32[]{:S(2)}) copy-start(bf16[8,32,128]{2,1,0:T(8,128)(2,1)} %fusion.15) | copy-start | bytes 196612
  260.5 533.0 %copy-start.2 = (bf16[64,32,32]{2,1,0:T(8,128)(2,1)S(1)}, bf16[64,32,32]{2,1,0:T(8,128)(2,1)}, u32[]{:S(2)}) copy-start(bf16[64,32,32]{2,1,0:T(8,128)(2,1)} %copy.43) | copy-start | bytes 393220
where the time goes:
time: 804 us; the launch traced here: 798 us
  other arithmetic  257 us (32%)
  matrix products  192 us (24%)
  local copies, waits for them, and re-layouts  180 us (22%)
  blocking collectives  144 us (18%)
  starting transfers between devices  24 us (3%)
    dot_general x27, matrix products, near_step(): jnp.einsum('lab,lbr->lar', kernel, other_charges, preferred_element_type=...  176 us
    reduce_sum x27, other arithmetic, near_step(): jnp.sum((points[:, :, :, None] - other_points[:, :, None, :]) ** 2, axis=0)  168 us
    gather x27, local copies, waits for them, and re-layouts, near_step(): other_charges = jnp.take(pool_charges, column, axis=0)  101 us
    all_gather x1, blocking collectives, per_device(): lax.all_gather(lifted.reshape(base_count, K * RHS), 'leaf', axis=0, tiled...  64.6 us
    gather x27, local copies, waits for them, and re-layouts, near_step(): other_points = jnp.take(pool_points, column, axis=1)  44.5 us
    psum x1, blocking collectives, per_device(): top_sum = lax.psum(top_partial, 'leaf')  40.9 us
    all_gather x1, blocking collectives, per_device(): lax.all_gather(base_coeffs.reshape(base_count, K * RHS), 'leaf', axis=0,...  38 us
    scatter-add x1, other arithmetic, per_device(): jax.ops.segment_sum(results.reshape(-1, K, RHS), local_ids, num_segments=...  31.1 us
  transfers between devices with their start and end apart: 6, of which 0 were waited for; matrix products, arithmetic and copies ran while one was open for 10% of the time, Pallas kernels for 0%

commit v1 on v0

--- a/solution.py
+++ b/solution.py
@@ -3,6 +3,7 @@
 import jax.numpy as jnp
 from jax import lax
 from jax.sharding import PartitionSpec as P
+from jax.lax import all_gather
 
 K = 32
 RHS = 128
@@ -110,7 +111,7 @@
         preferred_element_type=single_precision,
     )
     top_partial = jax.ops.segment_sum(top_products, top_target, num_segments=total_tops)
-    top_sum = lax.psum(top_partial, "leaf")
+    top_sum = jnp.sum(all_gather(top_partial, "leaf"), axis=0)
     top_field = top_sum.astype(bf16)
     targets = base_target[:, 0]
     per_cluster = max(2, 2 * NB // devices)

time: 804 us -> 748 us (0.930)
  local copies, waits for them, and re-layouts: 180 us -> 151 us
  blocking collectives: 144 us -> 115 us
  between operations: 0.38 us -> 13.9 us
    psum x1 -> x0, blocking collectives: 40.9 us -> none  [per_device(): top_sum = lax.psum(top_partial, 'leaf')]
    gather x27, local copies, waits for them, and re-layouts: 44.5 us -> 17.7 us  [near_step(): other_points = jnp.take(pool_points, column, axis=1)]
    all_gather x1, blocking collectives: 38 us -> 50.3 us  [per_device(): lax.all_gather(base_coeffs.reshape(base_count, K * RHS), 'leaf', axis=0,...]
  transfers between devices with their start and end apart: 6 -> 7, of which waited for: 0 -> 0; matrix products, arithmetic and copies ran while one was open for 10% -> 74% of each run, Pallas kernels for 0% -> 0%
where the time goes in v1:
time: 748 us; the launch traced here: 744 us
  other arithmetic  249 us (33%)
  matrix products  189 us (25%)
  local copies, waits for them, and re-layouts  151 us (20%)
  blocking collectives  115 us (15%)
  starting transfers between devices  24 us (3%)
  between operations  13.9 us (2%)
    dot_general x27, matrix products, near_step(): jnp.einsum('lab,lbr->lar', kernel, other_charges, preferred_element_type=...  175 us
    reduce_sum x27, other arithmetic, near_step(): jnp.sum((points[:, :, :, None] - other_points[:, :, None, :]) ** 2, axis=0)  164 us
    gather x27, local copies, waits for them, and re-layouts, near_step(): other_charges = jnp.take(pool_charges, column, axis=0)  101 us
    all_gather x1, blocking collectives, per_device(): lax.all_gather(lifted.reshape(base_count, K * RHS), 'leaf', axis=0, tiled...  65.2 us
    all_gather x1, blocking collectives, per_device(): lax.all_gather(base_coeffs.reshape(base_count, K * RHS), 'leaf', axis=0,...  50.3 us
    scatter-add x1, other arithmetic, per_device(): jax.ops.segment_sum(results.reshape(-1, K, RHS), local_ids, num_segments=...  31.1 us
    select_n x54, other arithmetic, near_step(): other_points = jnp.take(pool_points, column, axis=1)  22.4 us
    and x27, other arithmetic, near_step(): other_points = jnp.take(pool_points, column, axis=1)  19 us
  transfers between devices with their start and end apart: 7, of which 0 were waited for; matrix products, arithmetic and copies ran while one was open for 74% of the time, Pallas kernels for 0%

profile of v1, /device:TPU:0, one launch (start us, length us, event | category | flops | bytes accessed | tf_op | source)
XLA Modules:
  0.0 744.0 jit_solution(6390165756912751210)
XLA Ops:
  27.5 8.4 %all-to-all-start = ((s32[32,1,11]{2,1,0:T(1,128)}), s32[32,1,11]{2,1,0:T(1,128)S(1)}, u32[]{:S(2)}, u32[]{:S(2)}) async-start(s32[32,1,11]{2,1,0:T(1,128)} %bitcast.23), calls=%async_computation | async-start | bytes 32768 | tf_op jit(solution)/shard_map/all_to_all | solution.py:129
  39.9 65.2 %all-gather.1 = bf16[32,1,4096]{2,1,0:T(2,128)(2,1)S(1)} all-gather(bf16[1,1,4096]{2,1,0:T(2,128)(2,1)S(1)} %reshape.359), channel_id=1, replica_groups=mesh['leaf'=32] {'leaf'}, dimensions={0}, use_global_device_ids=true | all-gather | bytes 270336 | tf_op jit(solution)/shard_map/all_gather | solution.py:99
  119.3 50.3 %all-gather.2 = bf16[32,1,4096]{2,1,0:T(2,128)(2,1)S(1)} all-gather(bf16[1,1,4096]{2,1,0:T(2,128)(2,1)S(1)} %reshape.361), channel_id=1, replica_groups=mesh['leaf'=32] {'leaf'}, dimensions={0}, use_global_device_ids=true | all-gather | bytes 270336 | tf_op jit(solution)/shard_map/all_gather | solution.py:98
  183.0 6.2 fusion.10
  198.7 500.9 %while.12 = (s32[]{:T(128)}, f32[64,128,128]{2,1,0:T(8,128)}, f32[3,8192]{1,0:T(4,128)S(1)}, s32[27,64]{1,0:T(8,128)}, f32[3,192,128]{2,0,1:T(4,128)S(1)}, /*ind...) while((s32[]{:T(128)}, f32[64,128,128]{2,1,0:T(8,128)}, f32[3,8192]{1,0:T(4,128)S(1)}, ...), condition=%wide.region_2.3_spmd.clone, body=%wide.region_0.2_spmd.clone.sunk | while | flops 283141696 | bytes 24057648 | solution.py:42
  200.9 6.1 multiply_reduce_fusion.2
  218.2 6.1 multiply_reduce_fusion.2
  228.1 6.5 select_add_fusion.2
  246.7 6.5 select_add_fusion.2
  265.2 6.5 select_add_fusion.2
  274.0 6.1 multiply_reduce_fusion.2
  283.8 6.5 select_add_fusion.2
  302.4 6.5 select_add_fusion.2
  311.2 6.1 multiply_reduce_fusion.2
  321.0 6.5 select_add_fusion.2
  339.6 6.5 select_add_fusion.2
  348.4 6.1 multiply_reduce_fusion.2
  358.2 6.5 select_add_fusion.2
  367.0 6.1 multiply_reduce_fusion.2
  376.8 6.5 select_add_fusion.2
  385.6 6.1 multiply_reduce_fusion.2
  395.4 6.5 select_add_fusion.2
  404.2 6.1 multiply_reduce_fusion.2
  414.0 6.5 select_add_fusion.2
  432.6 6.5 select_add_fusion.2
  441.4 6.1 multiply_reduce_fusion.2
  451.2 6.5 select_add_fusion.2
  460.0 6.1 multiply_reduce_fusion.2
  469.8 6.5 select_add_fusion.2
  478.6 6.1 multiply_reduce_fusion.2
  488.4 6.5 select_add_fusion.2
  507.0 6.5 select_add_fusion.2
  525.6 6.5 select_add_fusion.2
  534.4 6.1 multiply_reduce_fusion.2
  544.2 6.5 select_add_fusion.2
  562.8 6.5 select_add_fusion.2
  571.6 6.1 multiply_reduce_fusion.2
  581.4 6.5 select_add_fusion.2
  590.2 6.1 multiply_reduce_fusion.2
  600.0 6.5 select_add_fusion.2
  618.6 6.5 select_add_fusion.2
  627.4 6.1 multiply_reduce_fusion.2
  637.2 6.5 select_add_fusion.2
  646.0 6.1 multiply_reduce_fusion.2
  655.8 6.5 select_add_fusion.2
  674.4 6.5 select_add_fusion.2
  693.0 6.5 select_add_fusion.2
  701.4 31.1 %scatter_fusion.1 = f32[32,128,1]{1,0,2:T(8,128)S(1)} fusion(f32[32,128,1]{1,0,2:T(8,128)S(1)} %convolution_bitcast_fusion.2, s32[352]{0:T(512)S(1)} %reshape.355, f32[352,32,128]{2,1,0:T(8,128)} %bitcast.137), kind=kCustom, calls=%fused_computation.7 | custom fusion | flops 1441792 | bytes 17302912 | tf_op jit(solution)/shard_map/scatter-add | solution.py:139
  (332 shorter events, 300.7 us)
Async XLA Ops:
  6.5 18.0 %copy-start.11 = (s32[189,1]{0,1:T(1,128)S(1)}, s32[189,1]{0,1:T(1,128)}, u32[]{:S(2)}) copy-start(s32[189,1]{0,1:T(1,128)} %param.23) | copy-start | bytes 2272
  6.5 29.5 %copy-start.8 = (bf16[64,4096]{1,0:T(8,128)(2,1)S(1)}, bf16[64,4096]{1,0:T(8,128)(2,1)}, u32[]{:S(2)}) copy-start(bf16[64,4096]{1,0:T(8,128)(2,1)} %param.18) | copy-start | bytes 1572868
  6.5 29.6 %copy-start.9 = (bf16[8,1024]{1,0:T(8,128)(2,1)S(1)}, bf16[8,1024]{1,0:T(8,128)(2,1)}, u32[]{:S(2)}) copy-start(bf16[8,1024]{1,0:T(8,128)(2,1)} %param.20) | copy-start | bytes 49156
  6.5 29.7 %copy-start.12 = (bf16[1,1024]{1,0:T(2,128)(2,1)S(1)}, bf16[1,1024]{1,0:T(2,128)(2,1)}, u32[]{:S(2)}) copy-start(bf16[1,1024]{1,0:T(2,128)(2,1)} %param.21) | copy-start | bytes 6148
  8.2 28.2 %copy-start.6 = (bf16[64,1024]{1,0:T(8,128)(2,1)S(1)}, bf16[64,1024]{1,0:T(8,128)(2,1)}, u32[]{:S(2)}) copy-start(bf16[64,1024]{1,0:T(8,128)(2,1)} %param.19) | copy-start | bytes 393220
  8.2 28.6 %copy-start = (bf16[8192,128]{1,0:T(8,128)(2,1)S(1)}, bf16[8192,128]{1,0:T(8,128)(2,1)}, u32[]{:S(2)}) copy-start(bf16[8192,128]{1,0:T(8,128)(2,1)} %param.16) | copy-start | bytes 6291460
  8.2 168.1 %collective-permute-start.1 = (f32[64,384]{1,0:T(8,128)}, f32[64,384]{1,0:T(8,128)}, u32[]{:S(2)}, u32[]{:S(2)}) collective-permute-start(f32[64,384]{1,0:T(8,128)} %bitcast.123), channel_id=1, source_target_pairs={{1,0},{2,1},{3,2},{4,3},{5,4},{6,5},{7,6},{8,7},{9,8},{10,9},{11,1... | collective-permute-start | bytes 294920 | tf_op jit(solution)/shard_map/ppermute | solution.py:23
  9.6 167.6 %collective-permute-start = (f32[64,384]{1,0:T(8,128)}, f32[64,384]{1,0:T(8,128)}, u32[]{:S(2)}, u32[]{:S(2)}) collective-permute-start(f32[64,384]{1,0:T(8,128)} %bitcast.123), channel_id=1, source_target_pairs={{0,1},{1,2},{2,3},{3,4},{4,5},{5,6},{6,7},{7,8},{8,9},{9,10},{10,1... | collective-permute-start | bytes 294920 | tf_op jit(solution)/shard_map/ppermute | solution.py:22
  17.4 171.8 %collective-permute-start.3 = (bf16[64,16384]{1,0:T(8,128)(2,1)}, bf16[64,16384]{1,0:T(8,128)(2,1)}, u32[]{:S(2)}, u32[]{:S(2)}) collective-permute-start(bf16[64,16384]{1,0:T(8,128)(2,1)} %reshape_reshape.3), channel_id=1, source_target_pairs={{1,0},{2,1},{3,2},{4,3},{5,4},{6,5},{7,6},{8,7},{9,8},{10,9},{11,1... | collective-permute-start | bytes 6291464 | tf_op jit(solution)/shard_map/ppermute | solution.py:23
  18.7 172.7 %collective-permute-start.2 = (bf16[64,16384]{1,0:T(8,128)(2,1)}, bf16[64,16384]{1,0:T(8,128)(2,1)}, u32[]{:S(2)}, u32[]{:S(2)}) collective-permute-start(bf16[64,16384]{1,0:T(8,128)(2,1)} %reshape_reshape.3), channel_id=1, source_target_pairs={{0,1},{1,2},{2,3},{3,4},{4,5},{5,6},{6,7},{7,8},{8,9},{9,10},{10,1... | collective-permute-start | bytes 6291464 | tf_op jit(solution)/shard_map/ppermute | solution.py:22
  27.5 84.1 %all-to-all-start = ((s32[32,1,11]{2,1,0:T(1,128)}), s32[32,1,11]{2,1,0:T(1,128)S(1)}, u32[]{:S(2)}, u32[]{:S(2)}) async-start(s32[32,1,11]{2,1,0:T(1,128)} %bitcast.23), calls=%async_computation | async-start | bytes 32768 | tf_op jit(solution)/shard_map/all_to_all | solution.py:129
  36.2 70.3 %copy-start.4 = (bf16[8,32,32]{2,1,0:T(8,128)(2,1)}, bf16[8,32,32]{2,1,0:T(8,128)(2,1)S(1)}, u32[]{:S(2)}) copy-start(bf16[8,32,32]{2,1,0:T(8,128)(2,1)S(1)} %reshape.231) | copy-start | bytes 49156
  36.7 69.9 %copy-start.14 = (s32[8]{0:T(128)S(1)}, s32[8]{0:T(128)}, u32[]{:S(2)}) copy-start(s32[8]{0:T(128)} %param.27) | copy-start | bytes 100
  105.0 10.1 %copy-start.10 = (bf16[8,1024]{1,0:T(8,128)(2,1)S(1)}, bf16[8,1024]{1,0:T(8,128)(2,1)}, u32[]{:S(2)}) copy-start(bf16[8,1024]{1,0:T(8,128)(2,1)} %param.25) | copy-start | bytes 49156
  106.6 9.5 %copy-start.13 = (s32[8]{0:T(128)S(1)}, s32[8]{0:T(128)}, u32[]{:S(2)}) copy-start(s32[8]{0:T(128)} %param.26) | copy-start | bytes 100
  109.4 8.1 %copy-start.7 = (bf16[64,1024]{1,0:T(8,128)(2,1)S(1)}, bf16[64,1024]{1,0:T(8,128)(2,1)}, u32[]{:S(2)}) copy-start(bf16[64,1024]{1,0:T(8,128)(2,1)} %param.19) | copy-start | bytes 393220
  111.7 66.6 %all-to-all-start.1 = ((bf16[32,11,1024]{2,1,0:T(8,128)(2,1)}), bf16[32,11,1024]{2,1,0:T(8,128)(2,1)}, u32[]{:S(2)}, u32[]{:S(2)}) async-start(bf16[32,11,1024]{2,1,0:T(8,128)(2,1)} %reshape.239), calls=%async_computation.1 | async-start | bytes 2097152 | tf_op jit(solution)/shard_map/all_to_all | solution.py:128
  115.0 584.5 %all-gather.5.cloned.1.call-start = ((), (), s32[]{:S(2)}) async-start(), calls=%async_computation.2 | async-start | bytes 2162688 | tf_op jit(solution)/shard_map/all_gather | solution.py:114
  116.9 0.6 copy-start.1
  173.2 5.0 copy-start.2
  701.4 31.1 %copy-start.5 = (bf16[8,32,32]{2,1,0:T(8,128)(2,1)S(1)}, bf16[8,32,32]{2,1,0:T(8,128)(2,1)}, u32[]{:S(2)}) copy-start(bf16[8,32,32]{2,1,0:T(8,128)(2,1)} %copy-done.4) | copy-start | bytes 49156
  701.4 31.3 %copy-start.3 = (bf16[64,32,32]{2,1,0:T(8,128)(2,1)S(1)}, bf16[64,32,32]{2,1,0:T(8,128)(2,1)}, u32[]{:S(2)}) copy-start(bf16[64,32,32]{2,1,0:T(8,128)(2,1)} %copy.43) | copy-start | bytes 393220
Sparse Core Ops, SparseCore 0:
  118.7 58.9 all-gather.4
